TPU v7x, 128 devices: a whole 4x4x4 slice. The times are simulated.
128 devices in a mesh: dp: 4 (over z_hi, core), ctx: 32 (over z_lo, y, x).
Axes of the slice: x: 4, y: 4, z: 4 (z_hi: 2, z_lo: 2; z = z_hi * 2 + z_lo), core: 2. Of those that a mesh axis runs over, the one named last changes fastest.
Arguments:
- density: float32 [512, 64, 64], P(('dp', 'ctx')), parts along dimension 0, may hold values from 0.1 to 50, as said below
- stem_weight: bfloat16 [216, 1024], replicated, may hold values from -0.4375 to 0.4375
- stem_bias: float32 [1024], replicated, may hold values from -3 to 3
- pos_embed: bfloat16 [8192, 1024], P('ctx'), may hold values from -3 to 3
- ln1_gain: float32 [1024], replicated, may hold values from 0.25 to 1.75
- ln1_bias: float32 [1024], replicated, may hold values from -2 to 2
- w_qkv: bfloat16 [1024, 3072], replicated, may hold values from -2 to 2
- qkv_bias: float32 [3072], replicated, may hold values from -2 to 2
- w_out: bfloat16 [1024, 1024], replicated, may hold values from -0.1875 to 0.1875
- out_bias: float32 [1024], replicated, may hold values from -2 to 2
- ln2_gain: float32 [1024], replicated, may hold values from 0.25 to 1.75
- ln2_bias: float32 [1024], replicated, may hold values from -2 to 2
- w_fc1: bfloat16 [1024, 4096], replicated, may hold values from -0.1875 to 0.1875
- fc1_bias: float32 [4096], replicated, may hold values from -3 to 3
- w_fc2: bfloat16 [4096, 1024], replicated, may hold values from -0.09375 to 0.09375
- fc2_bias: float32 [1024], replicated, may hold values from -2 to 2
Outputs:
- encoded: bfloat16 [32768, 1024], P(('dp', 'ctx')), parts along dimension 0
There are 4 independent parts, one for each index of `dp`. A program takes and returns all parts, laid end to end along the dimension named above; an argument that names none is the same for every part. Nothing has to cross between parts.
Inputs may be any that keep to these rules, and one draw needn't show every extreme that they name: density is positive.
All inputs are finite; a program needn't handle non-finite values.
Results may differ from a plain program's by a relative error of at most 0.013.
Values may be sent and summed in bfloat16 or wider, within the bound.
No kernel may reach another device: no remote copies, remote signals or barrier semaphores. Data moves between devices by JAX's collectives and lax.ppermute only.
A program may use at most 384 MiB of HBM per device.

v0:
```python
import functools
import math

import jax
import jax.numpy as jnp
from jax import lax
from jax.experimental import pallas as pl
from jax.experimental.pallas import tpu as pltpu
from jax.sharding import PartitionSpec as P

HEADS = 16
HEAD = 64
D = 1024
FF = 4096
SIDE = 16
TOK = 256
PLANE = 16
BOUND = 100.0
F32 = jnp.float32
BF16 = jnp.bfloat16


def layer_norm(values, gain, shift):
    center = values - jnp.mean(values, axis=-1, keepdims=True)
    spread = jnp.mean(center * center, axis=-1, keepdims=True)
    return center * lax.rsqrt(spread + 1e-06) * gain + shift


def front_kernel(
    sums_ref, edge_ref, low_ref, mid_ref, high_ref, pick_ref, stem_ref, sbias_ref, pos_ref,
    gain_ref, shift_ref, wqkv_ref, qbias_ref, send_ref, resid_ref, cols_ref,
):
    total = jnp.sum(sums_ref[...])
    mean = total / (32 * 4 * 64 * 64)
    planes = []
    for a in range(6):
        if a == 0:
            values = jnp.where(edge_ref[0] > 0, low_ref[0], mean)
        elif a == 5:
            values = jnp.where(edge_ref[1] > 0, high_ref[0], mean)
        else:
            values = mid_ref[a - 1]
        planes.append(jnp.log(values / mean).astype(BF16))
    field = jnp.concatenate(planes, axis=0)
    cols_ref[:, 0:8, :] = jnp.zeros((SIDE, 8, 128), F32)
    cols_ref[:, 72:80, :] = jnp.zeros((SIDE, 8, 128), F32)
    picked = lax.dot_general(
        field, pick_ref[...], (((0,), (0,)), ((), ())), preferred_element_type=F32
    )
    for j in range(SIDE):
        cols_ref[j, 8:72, :] = picked[:, j * 128 : (j + 1) * 128]
    embedded = sbias_ref[...] + pos_ref[...].astype(F32)
    for c in range(6):
        rows = [cols_ref[j, pl.ds(7 + c, SIDE, stride=4), :] for j in range(SIDE)]
        taps = jnp.concatenate(rows, axis=0).astype(BF16)
        embedded = embedded + jnp.dot(taps[:, :48], stem_ref[c], preferred_element_type=F32)
    residual = embedded.astype(BF16)
    resid_ref[...] = residual
    normed = layer_norm(residual.astype(F32), gain_ref[...], shift_ref[...]).astype(BF16)
    scale = math.log2(math.e) / math.sqrt(HEAD)
    place = (2, 0, 1)
    for part in range(3):
        for n in range(2):
            start = part * D + n * 512
            out = jnp.dot(normed, wqkv_ref[:, start : start + 512], preferred_element_type=F32)
            out = out + qbias_ref[:, start : start + 512]
            if part == 0:
                out = out * scale
            out = out.astype(BF16)
            for h in range(0, 8, 2):
                pair = out[:, h * HEAD : (h + 2) * HEAD].T
                row = place[part] * HEAD
                send_ref[n * 8 + h, row : row + HEAD, :] = pair[:HEAD]
                send_ref[n * 8 + h + 1, row : row + HEAD, :] = pair[HEAD:]


def largest_square(ref, first):
    def one(s, best):
        values = ref[s, first : first + HEAD, :].astype(F32)
        return jnp.maximum(best, jnp.sum(values * values, axis=0, keepdims=True))

    return jnp.max(lax.fori_loop(0, PLANE, one, jnp.zeros((1, TOK), F32)))


def attend_kernel(*refs, last):
    if last:
        (q_ref, kv_ref, acc_in, max_in, out_ref, k_scr, v_scr, flag) = refs
    else:
        (q_ref, acc_out, max_out, k_scr, v_scr, flag) = refs
        kv_ref = q_ref
    step = pl.program_id(0)

    @pl.when(step == 0)
    def _():
        def one(s, _):
            off = pl.multiple_of(s * TOK, TOK)
            k_scr[pl.ds(off, TOK), :] = kv_ref[s, 0:HEAD, :].T
            v_scr[0:HEAD, pl.ds(off, TOK)] = kv_ref[s, HEAD : 2 * HEAD, :]
            return 0

        lax.fori_loop(0, PLANE, one, 0)
        v_scr[HEAD : HEAD + 16, :] = jnp.ones((16, PLANE * TOK), BF16)
        reach = largest_square(kv_ref, 0) * largest_square(q_ref, 2 * HEAD)
        flag[0] = jnp.where(reach <= BOUND * BOUND, 1, 0).astype(jnp.int32)

    small = flag[0] == 1
    row = 2 * HEAD
    query = jnp.concatenate(
        [q_ref[2 * step, row : row + HEAD, :], q_ref[2 * step + 1, row : row + HEAD, :]], axis=1
    )
    width = 2 * TOK

    def finish(acc, top):
        if last:
            out = (acc[:HEAD] / acc[HEAD : HEAD + 1]).astype(BF16)
            out_ref[0] = out[:, :TOK]
            out_ref[1] = out[:, TOK:]
        else:
            acc_out[...] = acc
            max_out[...] = top

    if last:
        carried = jnp.all(max_in[...] == 0.0)
        plain = jnp.logical_and(small, carried)
    else:
        plain = small

    @pl.when(plain)
    def _():
        scores = jnp.dot(k_scr[...], query, preferred_element_type=F32)
        weights = jnp.exp2(scores).astype(BF16)
        acc = jnp.dot(v_scr[...], weights, preferred_element_type=F32)
        if last:
            acc = acc + acc_in[...]
        finish(acc, jnp.zeros((8, width), F32))

    @pl.when(jnp.logical_not(plain))
    def _():
        chunk = 256

        def one(c, carry):
            acc, top = carry
            off = pl.multiple_of(c * chunk, chunk)
            scores = jnp.dot(k_scr[pl.ds(off, chunk), :], query, preferred_element_type=F32)
            new_top = jnp.maximum(top, jnp.max(scores, axis=0, keepdims=True))
            weights = jnp.exp2(scores - new_top).astype(BF16)
            acc = acc * jnp.exp2(top - new_top) + jnp.dot(
                v_scr[:, pl.ds(off, chunk)], weights, preferred_element_type=F32
            )
            return acc, new_top

        if last:
            begin = (acc_in[...], max_in[0:1, :])
        else:
            begin = (jnp.zeros((HEAD + 16, width), F32), jnp.full((1, width), -3e38, F32))
        acc, top = lax.fori_loop(0, PLANE * TOK // chunk, one, begin)
        finish(acc, jnp.broadcast_to(top, (8, width)))


def attend(operands, last):
    width = 2 * TOK
    queries = PLANE * TOK
    whole = lambda rows: pl.BlockSpec((PLANE, rows, TOK), lambda i: (0, 0, 0))
    acc_spec = pl.BlockSpec((HEAD + 16, width), lambda i: (0, i))
    max_spec = pl.BlockSpec((8, width), lambda i: (0, i))
    if last:
        in_specs = [whole(3 * HEAD), whole(2 * HEAD), acc_spec, max_spec]
        out_specs = pl.BlockSpec((2, HEAD, TOK), lambda i: (i, 0, 0))
        out_shape = jax.ShapeDtypeStruct((PLANE, HEAD, TOK), BF16)
    else:
        in_specs = [whole(3 * HEAD)]
        out_specs = [acc_spec, max_spec]
        out_shape = [
            jax.ShapeDtypeStruct((HEAD + 16, queries), F32),
            jax.ShapeDtypeStruct((8, queries), F32),
        ]
    return pl.pallas_call(
        functools.partial(attend_kernel, last=last),
        grid=(queries // width,),
        in_specs=in_specs,
        out_specs=out_specs,
        out_shape=out_shape,
        scratch_shapes=[
            pltpu.VMEM((queries, HEAD), BF16),
            pltpu.VMEM((HEAD + 16, queries), BF16),
            pltpu.SMEM((1,), jnp.int32),
        ],
        compiler_params=pltpu.CompilerParams(vmem_limit_bytes=24 * 2**20),
        name="attend_last" if last else "attend_first",
    )(*operands)


def back_kernel(
    att_ref, resid_ref, wout_ref, obias_ref, gain_ref, shift_ref, fc1_ref, b1_ref, fc2_ref,
    b2_ref, out_ref,
):
    mixed = lax.dot_general(
        att_ref[...], wout_ref[...], (((0,), (0,)), ((), ())), preferred_element_type=F32
    )
    stream = (resid_ref[...].astype(F32) + mixed + obias_ref[...]).astype(BF16)
    wide = stream.astype(F32)
    normed = layer_norm(wide, gain_ref[...], shift_ref[...]).astype(BF16)
    acc = wide + b2_ref[...]
    chunk = 1024
    for f in range(0, FF, chunk):
        pre = jnp.dot(normed, fc1_ref[:, f : f + chunk], preferred_element_type=F32)
        pre = pre + b1_ref[:, f : f + chunk]
        hidden = (0.5 * pre * (1.0 + lax.erf(pre * math.sqrt(0.5)))).astype(BF16)
        acc = acc + jnp.dot(hidden, fc2_ref[f : f + chunk, :], preferred_element_type=F32)
    out_ref[...] = acc.astype(BF16)


def call_whole(kernel, operands, out_shape, name, scratch=(), limit=40, smem=()):
    specs = [
        pl.BlockSpec(memory_space=pltpu.SMEM if i in smem else pltpu.VMEM)
        for i in range(len(operands))
    ]
    many = isinstance(out_shape, (list, tuple))
    out_specs = pl.BlockSpec(memory_space=pltpu.VMEM)
    return pl.pallas_call(
        kernel,
        in_specs=specs,
        out_specs=[out_specs] * len(out_shape) if many else out_specs,
        out_shape=out_shape,
        scratch_shapes=list(scratch),
        compiler_params=pltpu.CompilerParams(vmem_limit_bytes=limit * 2**20),
        name=name,
    )(*operands)


def picker():
    row = lax.broadcasted_iota(jnp.int32, (384, 2048), 0)
    col = lax.broadcasted_iota(jnp.int32, (384, 2048), 1)
    tap = col % 128
    hit = (row // 64 == tap // 6) & (row % 64 == 4 * (col // 128) - 1 + tap % 6)
    return hit.astype(BF16)


def per_device(
    density, stem_weight, stem_bias, pos_embed, ln1_gain, ln1_bias, w_qkv, qkv_bias, w_out,
    out_bias, ln2_gain, ln2_bias, w_fc1, fc1_bias, w_fc2, fc2_bias,
):
    axis = "ctx"
    index = lax.axis_index(axis)
    local = jnp.sum(density)
    sums = lax.all_to_all(
        jnp.broadcast_to(local, (32, 1, 1)), axis, split_axis=0, concat_axis=0, tiled=True
    ).reshape(1, 32)
    up = [(i, i + 1) for i in range(31)]
    low = lax.ppermute(density[3:4], axis, up)
    high = lax.ppermute(density[0:1], axis, [(b, a) for a, b in up])
    edge = jnp.stack([index > 0, index < 31]).astype(jnp.int32)
    stem = stem_weight.reshape(36, 6, D).transpose(1, 0, 2)
    stem = jnp.pad(stem, ((0, 0), (0, 12), (0, 0)))
    row = lambda v: v.reshape(1, -1)
    send, residual = call_whole(
        front_kernel,
        (sums, edge, low, density, high, picker(), stem, row(stem_bias), pos_embed,
         row(ln1_gain), row(ln1_bias), w_qkv, row(qkv_bias)),
        [
            jax.ShapeDtypeStruct((PLANE, 3 * HEAD, TOK), BF16),
            jax.ShapeDtypeStruct((TOK, D), BF16),
        ],
        "front",
        scratch=(pltpu.VMEM((SIDE, 80, 128), F32),),
        smem=(1,),
    )
    groups = [list(range(PLANE)), list(range(PLANE, 2 * PLANE))]
    got = lax.all_to_all(
        send, axis, split_axis=0, concat_axis=0, tiled=True, axis_index_groups=groups
    )
    other = lax.ppermute(got[:, : 2 * HEAD, :], axis, [(i, i ^ PLANE) for i in range(32)])
    acc, top = attend((got,), False)
    mixed = attend((got, other, acc, top), True)
    back = lax.all_to_all(
        mixed, axis, split_axis=0, concat_axis=0, tiled=True, axis_index_groups=groups
    )
    return call_whole(
        back_kernel,
        (back.reshape(D, TOK), residual, w_out, row(out_bias), row(ln2_gain), row(ln2_bias),
         w_fc1, row(fc1_bias), w_fc2, row(fc2_bias)),
        jax.ShapeDtypeStruct((TOK, D), BF16),
        "back",
    )


def solution(mesh):
    in_specs = (
        P(("dp", "ctx"), None, None),
        P(), P(),
        P("ctx", None),
        P(), P(), P(), P(), P(), P(), P(), P(), P(), P(), P(), P(),
    )
    return jax.shard_map(
        per_device, mesh=mesh, in_specs=in_specs, out_specs=P(("dp", "ctx"), None), check_vma=False
    )
```

profile of v0, /device:TPU:0, one launch (start us, length us, event | category | flops | bytes accessed | tf_op | source)
XLA Modules:
  0.0 205.1 jit_solution(14343843129593854291)
XLA Ops:
  0.0 1.7 reduce_sum.9
  1.7 1.3 broadcast_in_dim.3
  3.0 8.8 %all-to-all-start = ((f32[32,1,1]{2,1,0:T(1,128)}), f32[32,1,1]{2,1,0:T(1,128)S(1)}, u32[]{:S(2)}, u32[]{:S(2)}) async-start(f32[32,1,1]{2,1,0:T(1,128)} %broadcast_in_dim.3), calls=%async_computation | async-start | bytes 32768 | tf_op jit(solution)/shard_map/all_to_all | solution.py:246
  11.8 0.8 fusion.24
  12.6 1.3 collective-permute-start.1
  13.9 4.5 %collective-permute-start = (f32[1,64,64]{2,1,0:T(8,128)S(1)}, f32[1,64,64]{2,1,0:T(8,128)S(1)}, u32[]{:S(2)}, u32[]{:S(2)}) collective-permute-start(f32[1,64,64]{2,1,0:T(8,128)S(1)} %get-tuple-element.14), channel_id=1, source_target_pairs={{0,1},{1,2},{2,3},{3,4},{4,5},{5,6},{6,7},{7,8},{8,9},{9,10},{10,1... | collective-permute-start | bytes 49160 | tf_op jit(solution)/shard_map/ppermute | solution.py:250
  18.6 1.2 fusion.11.pick_ref
  19.7 0.1 add_convert_fusion.edge_ref
  19.8 1.2 reshape.37
  21.0 0.2 copy.21
  21.2 0.1 pad.4.stem_ref
  21.3 0.0 all-to-all-done
  21.3 0.3 reduce
  21.6 0.0 collective-permute-done.1.high_ref
  21.7 0.0 copy-start
  21.7 2.8 %copy-done = bf16[1024,3072]{1,0:T(8,128)(2,1)S(1)} copy-done((bf16[1024,3072]{1,0:T(8,128)(2,1)S(1)}, bf16[1024,3072]{1,0:T(8,128)(2,1)}, u32[]{:S(2)}) %copy-start) | copy-done | bytes 6291480
  24.5 4.2 %front.1 = (bf16[16,192,256]{2,1,0:T(8,128)(2,1)S(1)}, bf16[256,1024]{1,0:T(8,128)(2,1)S(1)}) custom-call(f32[1,32]{1,0:T(1,128)S(1)} %bitcast.28, s32[2]{0:T(128)S(1)} %add_convert_fusion.edge_ref, f32[1,64,64]{2,1,0:T(8,128)S(1)} %collective-permute-done.low_ref, f32[4,64,64]{2,1,0:T(8,128)S(1)} %copy-done.2, ...), custom_call_target="tpu_custom_call" | custom-call | tf_op jit(solution)/shard_map/front/pallas_call | solution.py:220
  28.7 0.0 slice-start.1
  28.7 32.7 %all_to_all.15.refs_0_ = bf16[16,192,256]{2,1,0:T(8,128)(2,1)S(1)} all-to-all(bf16[16,192,256]{2,1,0:T(8,128)(2,1)S(1)} %get-tuple-element.9), channel_id=1, replica_groups={{0,1,2,3,4,5,6,7,8,9,10,11,12,13,14,15},{16,17,18,19,20,21,22,23,24,25,..., dimensions={0} | all-to-all | bytes 3145728 | tf_op jit(solution)/shard_map/all_to_all | solution.py:269
  61.4 0.1 slice.12
  61.5 0.9 collective-permute-start.2
  62.4 17.6 %attend_first.1 = (f32[80,4096]{1,0:T(8,128)S(1)}, f32[8,4096]{1,0:T(8,128)S(1)}) custom-call(bf16[16,192,256]{2,1,0:T(8,128)(2,1)S(1)} %all_to_all.15.refs_0_), custom_call_target="tpu_custom_call" | custom-call | tf_op jit(solution)/shard_map/attend_first/pallas_call | solution.py:177
  80.0 0.0 copy-start.1
  80.0 0.0 copy-start.4
  80.0 0.0 copy-start.9
  80.1 0.0 copy-start.10
  80.1 0.0 copy-start.11
  80.1 0.0 copy-start.12
  80.1 4.1 %collective-permute-done.2.refs_1_ = bf16[16,128,256]{2,1,0:T(8,128)(2,1)S(1)} collective-permute-done((bf16[16,128,256]{2,1,0:T(8,128)(2,1)S(1)}, bf16[16,128,256]{2,1,0:T(8,128)(2,1)S(1)}, u32[]{:S(2)}, u32[]{:S(2)}) %collective-permute-start.2) | collective-permute-done | bytes 1048608 | tf_op jit(solution)/shard_map/ppermute | solution.py:272
  84.2 59.4 %attend_last.1 = bf16[16,64,256]{2,1,0:T(8,128)(2,1)S(1)} custom-call(bf16[16,192,256]{2,1,0:T(8,128)(2,1)S(1)} %all_to_all.15.refs_0_, bf16[16,128,256]{2,1,0:T(8,128)(2,1)S(1)} %collective-permute-done.2.refs_1_, f32[80,4096]{1,0:T(8,128)S(1)} %get-tuple-element.10.refs_2_, f32[8,4096]{1,0:T(8,128)S(1)} %get-tuple-element.11.refs_3_), custom_call_target="tpu_custom_call" | custom-call | tf_op jit(solution)/shard_map/attend_last/pallas_call | solution.py:177
  143.6 51.6 %all_to_all.16 = bf16[16,64,256]{2,1,0:T(8,128)(2,1)S(1)} all-to-all(bf16[16,64,256]{2,1,0:T(8,128)(2,1)S(1)} %attend_last.1), channel_id=1, replica_groups={{0,1,2,3,4,5,6,7,8,9,10,11,12,13,14,15},{16,17,18,19,20,21,22,23,24,25,..., dimensions={0} | all-to-all | bytes 1048576 | tf_op jit(solution)/shard_map/all_to_all | solution.py:275
  195.3 9.8 %back.1 = bf16[256,1024]{1,0:T(8,128)(2,1)} custom-call(bf16[1024,256]{1,0:T(8,128)(2,1)S(1)} %bitcast.18, bf16[256,1024]{1,0:T(8,128)(2,1)S(1)} %get-tuple-element.12.resid_ref, bf16[1024,1024]{1,0:T(8,128)(2,1)S(1)} %copy-done.1, f32[1,1024]{1,0:T(1,128)S(1)} %bitcast.24, f32[1,1024]{1,0:T(1,128)S(1)} %bitcast.25, f32[1,1024]{1,0:T(1,128)S(1)} %bitcast.26, ...), custom_call_target="tpu_custom_call" | custom-call | tf_op jit(solution)/shard_map/back/pallas_call | solution.py:220
  (29 shorter events, 0.1 us)
Async XLA Ops:
  0.0 21.6 %copy-start.2 = (f32[4,64,64]{2,1,0:T(8,128)S(1)}, f32[4,64,64]{2,1,0:T(8,128)}, u32[]{:S(2)}) copy-start(f32[4,64,64]{2,1,0:T(8,128)} %mid_ref.1) | copy-start | bytes 196612
  0.0 21.6 %copy-start.5 = (f32[3072]{0:T(1024)S(1)}, f32[3072]{0:T(1024)}, u32[]{:S(2)}) copy-start(f32[3072]{0:T(1024)} %param.23) | copy-start | bytes 36868
  0.0 21.6 %copy-start.8 = (f32[1024]{0:T(1024)S(1)}, f32[1024]{0:T(1024)}, u32[]{:S(2)}) copy-start(f32[1024]{0:T(1024)} %param.21) | copy-start | bytes 12292
  0.0 21.7 %copy-start.7 = (f32[1024]{0:T(1024)S(1)}, f32[1024]{0:T(1024)}, u32[]{:S(2)}) copy-start(f32[1024]{0:T(1024)} %param.20) | copy-start | bytes 12292
  0.0 21.7 %copy-start.3 = (bf16[256,1024]{1,0:T(8,128)(2,1)S(1)}, bf16[256,1024]{1,0:T(8,128)(2,1)}, u32[]{:S(2)}) copy-start(bf16[256,1024]{1,0:T(8,128)(2,1)} %pos_ref.1) | copy-start | bytes 1572868
  0.0 21.7 %copy-start.6 = (f32[1024]{0:T(1024)S(1)}, f32[1024]{0:T(1024)}, u32[]{:S(2)}) copy-start(f32[1024]{0:T(1024)} %param.18) | copy-start | bytes 12292
  3.0 18.3 %all-to-all-start = ((f32[32,1,1]{2,1,0:T(1,128)}), f32[32,1,1]{2,1,0:T(1,128)S(1)}, u32[]{:S(2)}, u32[]{:S(2)}) async-start(f32[32,1,1]{2,1,0:T(1,128)} %broadcast_in_dim.3), calls=%async_computation | async-start | bytes 32768 | tf_op jit(solution)/shard_map/all_to_all | solution.py:246
  12.6 9.0 %collective-permute-start.1 = (f32[1,64,64]{2,1,0:T(8,128)S(1)}, f32[1,64,64]{2,1,0:T(8,128)S(1)}, u32[]{:S(2)}, u32[]{:S(2)}) collective-permute-start(f32[1,64,64]{2,1,0:T(8,128)S(1)} %get-tuple-element.13), channel_id=1, source_target_pairs={{1,0},{2,1},{3,2},{4,3},{5,4},{6,5},{7,6},{8,7},{9,8},{10,9},{11,1... | collective-permute-start | bytes 49160 | tf_op jit(solution)/shard_map/ppermute | solution.py:251
  13.9 7.7 %collective-permute-start = (f32[1,64,64]{2,1,0:T(8,128)S(1)}, f32[1,64,64]{2,1,0:T(8,128)S(1)}, u32[]{:S(2)}, u32[]{:S(2)}) collective-permute-start(f32[1,64,64]{2,1,0:T(8,128)S(1)} %get-tuple-element.14), channel_id=1, source_target_pairs={{0,1},{1,2},{2,3},{3,4},{4,5},{5,6},{6,7},{7,8},{8,9},{9,10},{10,1... | collective-permute-start | bytes 49160 | tf_op jit(solution)/shard_map/ppermute | solution.py:250
  21.7 2.8 %copy-start = (bf16[1024,3072]{1,0:T(8,128)(2,1)S(1)}, bf16[1024,3072]{1,0:T(8,128)(2,1)}, u32[]{:S(2)}) copy-start(bf16[1024,3072]{1,0:T(8,128)(2,1)} %wqkv_ref.1) | copy-start | bytes 18874372
  24.5 170.7 %slice-start = ((s8[8388608]{0:T(1024)(128)(4,1)}), s8[4194304]{0:T(1024)(128)(4,1)S(1)}, s32[]{:S(2)}) async-start(s8[8388608]{0:T(1024)(128)(4,1)} %bitcast.16), calls=%async_computation.3 | async-start | bytes 8388608
  28.7 166.6 %slice-start.1 = ((s8[8388608]{0:T(1024)(128)(4,1)}), s8[4194304]{0:T(1024)(128)(4,1)S(1)}, s32[]{:S(2)}) async-start(s8[8388608]{0:T(1024)(128)(4,1)} %bitcast.16), calls=%async_computation.4 | async-start | bytes 8388608
  61.5 22.7 %collective-permute-start.2 = (bf16[16,128,256]{2,1,0:T(8,128)(2,1)S(1)}, bf16[16,128,256]{2,1,0:T(8,128)(2,1)S(1)}, u32[]{:S(2)}, u32[]{:S(2)}) collective-permute-start(bf16[16,128,256]{2,1,0:T(8,128)(2,1)S(1)} %slice.12), channel_id=1, source_target_pairs={{0,16},{1,17},{2,18},{3,19},{4,20},{5,21},{6,22},{7,23},{8,24},{9,... | collective-permute-start | bytes 3145736 | tf_op jit(solution)/shard_map/ppermute | solution.py:272
  80.0 115.2 %copy-start.1 = (bf16[1024,1024]{1,0:T(8,128)(2,1)S(1)}, bf16[1024,1024]{1,0:T(8,128)(2,1)}, u32[]{:S(2)}) copy-start(bf16[1024,1024]{1,0:T(8,128)(2,1)} %wout_ref.1) | copy-start | bytes 6291460
  80.0 115.2 %copy-start.4 = (f32[4096]{0:T(1024)S(1)}, f32[4096]{0:T(1024)}, u32[]{:S(2)}) copy-start(f32[4096]{0:T(1024)} %param.29) | copy-start | bytes 49156
  80.0 115.2 %copy-start.9 = (f32[1024]{0:T(1024)S(1)}, f32[1024]{0:T(1024)}, u32[]{:S(2)}) copy-start(f32[1024]{0:T(1024)} %param.25) | copy-start | bytes 12292
  80.1 115.2 %copy-start.10 = (f32[1024]{0:T(1024)S(1)}, f32[1024]{0:T(1024)}, u32[]{:S(2)}) copy-start(f32[1024]{0:T(1024)} %param.26) | copy-start | bytes 12292
  80.1 115.2 %copy-start.11 = (f32[1024]{0:T(1024)S(1)}, f32[1024]{0:T(1024)}, u32[]{:S(2)}) copy-start(f32[1024]{0:T(1024)} %param.27) | copy-start | bytes 12292
  80.1 115.2 %copy-start.12 = (f32[1024]{0:T(1024)S(1)}, f32[1024]{0:T(1024)}, u32[]{:S(2)}) copy-start(f32[1024]{0:T(1024)} %param.31) | copy-start | bytes 12292
where the time goes:
time: 206 us; the launch traced here: 205 us
  Pallas kernels  90.9 us (44%)
  blocking collectives  84.3 us (41%)
  starting transfers between devices  15.6 us (8%)
  local copies, waits for them, and re-layouts  6.49 us (3%)
  waiting for transfers between devices  4.14 us (2%)
  other arithmetic  3.28 us (2%)
    pallas_call x2, Pallas kernels, attend(): pl.pallas_call(functools.partial(attend_kernel, last=last), grid=(queries...  76.9 us
    all_to_all x1, blocking collectives, per_device(): lax.all_to_all(mixed, axis, split_axis=0, concat_axis=0, tiled=True, axis...  51.6 us
    all_to_all x1, blocking collectives, per_device(): lax.all_to_all(send, axis, split_axis=0, concat_axis=0, tiled=True, axis_...  32.7 us
    pallas_call x2, Pallas kernels, call_whole(): pl.pallas_call(kernel, in_specs=specs, out_specs=[out_specs] * len(out_sh...  14 us
    all_to_all x1, starting transfers between devices, per_device(): lax.all_to_all(jnp.broadcast_to(local, (32, 1, 1)), axis, split_axis=0, c...  8.83 us
    ppermute x1, starting transfers between devices, per_device(): low = lax.ppermute(density[3:4], axis, up)  4.55 us
    ppermute x1, waiting for transfers between devices, per_device(): lax.ppermute(got[:, :2 * HEAD, :], axis, [(i, i ^ PLANE) for i in range(3...  4.14 us
  transfers between devices with their start and end apart: 4, of which 1 were waited for; matrix products, arithmetic and copies ran while one was open for 2% of the time, Pallas kernels for 9%

commit v1 on v0

v1 whole, which is shorter than its diff:
```python
import math

import jax
import jax.numpy as jnp
from jax import lax
from jax.experimental import pallas as pl
from jax.experimental.pallas import tpu as pltpu
from jax.sharding import PartitionSpec as P

HEADS = 16
HEAD = 64
D = 1024
FF = 4096
SIDE = 16
TOK = 256
DEVS = 32
BOUND = 100.0
F32 = jnp.float32
BF16 = jnp.bfloat16


def layer_norm(values, gain, shift):
    center = values - jnp.mean(values, axis=-1, keepdims=True)
    spread = jnp.mean(center * center, axis=-1, keepdims=True)
    return center * lax.rsqrt(spread + 1e-06) * gain + shift


def start_kernel(index_ref, density_ref, out_ref):
    index = index_ref[0]
    total = jnp.sum(density_ref[...]) * jnp.ones((8, 128), F32)

    def packed(plane):
        return jnp.concatenate([plane[:32], plane[32:]], axis=1)

    bottom = packed(density_ref[0])
    for d in range(DEVS):
        out_ref[d, 0:32, :] = bottom
        out_ref[d, 32:40, :] = total

    @pl.when(index < DEVS - 1)
    def _():
        out_ref[index + 1, 0:32, :] = packed(density_ref[3])


def front_kernel(
    index_ref, got_ref, mid_ref, stem_ref, sbias_ref, pos_ref, gain_ref, shift_ref, qbias_ref,
    wqkv_hbm, send_ref, resid_ref, cols_ref, pick_ref, wqkv_ref, sems,
):
    copies = [
        pltpu.make_async_copy(
            wqkv_hbm.at[:, pl.ds(n * 512, 512)], wqkv_ref.at[n], sems.at[n]
        )
        for n in range(6)
    ]
    for copy in copies:
        copy.start()
    index = index_ref[0]
    row = lax.broadcasted_iota(jnp.int32, (64, 2048), 0)
    col = lax.broadcasted_iota(jnp.int32, (64, 2048), 1)
    tap = col % 128
    hit = row == 4 * (col // 128) - 1 + tap % 6
    for a in range(6):
        chosen = jnp.where(tap // 6 == a, jnp.where(hit, 1.0, 0.0), 0.0)
        pick_ref[a * 64 : (a + 1) * 64, :] = chosen.astype(BF16)
    row = lax.broadcasted_iota(jnp.int32, (288, 216), 0)
    col = lax.broadcasted_iota(jnp.int32, (288, 216), 1)
    order = jnp.where((row % 48 < 36) & (col == (row % 48) * 6 + row // 48), 1.0, 0.0)
    stem = jnp.dot(order.astype(BF16), stem_ref[...], preferred_element_type=F32).astype(BF16)

    total = jnp.sum(got_ref[:, 32:33, :], axis=0)
    mean = total[:, 0:64] / (DEVS * 4 * 64 * 64)

    def halo(source, valid):
        block = got_ref[source, 0:32, :]
        plane = jnp.concatenate([block[:, :64], block[:, 64:]], axis=0)
        return jnp.where(valid, plane, mean)

    low = halo(jnp.maximum(index - 1, 0), index > 0)
    high = halo(jnp.minimum(index + 1, DEVS - 1), index < DEVS - 1)
    planes = [low] + [mid_ref[a] for a in range(4)] + [high]
    field = jnp.concatenate([jnp.log(p / mean).astype(BF16) for p in planes], axis=0)
    cols_ref[:, 0:8, :] = jnp.zeros((SIDE, 8, 128), F32)
    cols_ref[:, 72:80, :] = jnp.zeros((SIDE, 8, 128), F32)
    picked = lax.dot_general(
        field, pick_ref[...], (((0,), (0,)), ((), ())), preferred_element_type=F32
    )
    for j in range(SIDE):
        cols_ref[j, 8:72, :] = picked[:, j * 128 : (j + 1) * 128]
    embedded = sbias_ref[...] + pos_ref[...].astype(F32)
    for c in range(6):
        rows = [cols_ref[j, pl.ds(7 + c, SIDE, stride=4), :] for j in range(SIDE)]
        taps = jnp.concatenate(rows, axis=0).astype(BF16)
        embedded = embedded + jnp.dot(
            taps[:, :48], stem[c * 48 : (c + 1) * 48], preferred_element_type=F32
        )
    residual = embedded.astype(BF16)
    resid_ref[...] = residual
    normed = layer_norm(residual.astype(F32), gain_ref[...], shift_ref[...]).astype(BF16)
    scale = math.log2(math.e) / math.sqrt(HEAD)
    for part in range(3):
        for n in range(2):
            start = part * D + n * 512
            copies[part * 2 + n].wait()
            out = jnp.dot(normed, wqkv_ref[part * 2 + n], preferred_element_type=F32)
            out = out + qbias_ref[:, start : start + 512]
            if part == 0:
                out = out * scale
            out = out.astype(BF16)
            for pair in range(4):
                both = out[:, pair * 128 : (pair + 1) * 128].T
                for half in range(2):
                    head = n * 8 + pair * 2 + half
                    block = both[half * HEAD : (half + 1) * HEAD]
                    left, right = block[:, :128], block[:, 128:]
                    if part == 0:
                        send_ref[head, 256:320, :] = left
                        send_ref[head + HEADS, 256:320, :] = right
                    else:
                        base = (part - 1) * 128
                        for g in range(2):
                            send_ref[head + g * HEADS, base : base + 64, :] = left
                            send_ref[head + g * HEADS, base + 64 : base + 128, :] = right


def attend_kernel(got_ref, out_ref, k_scr, v_scr):
    zero = jnp.zeros((1, 128), F32)
    reach_k, reach_q = zero, zero

    def square(block):
        wide = block.astype(F32)
        return jnp.sum(wide * wide, axis=0, keepdims=True)

    for s in range(DEVS):
        key = jnp.concatenate([got_ref[s, 0:64, :], got_ref[s, 64:128, :]], axis=1)
        k_scr[s * TOK : (s + 1) * TOK, :] = key.T
        v_scr[0:HEAD, s * TOK : s * TOK + 128] = got_ref[s, 128:192, :]
        v_scr[0:HEAD, s * TOK + 128 : (s + 1) * TOK] = got_ref[s, 192:256, :]
        reach_k = jnp.maximum(reach_k, square(got_ref[s, 0:64, :]))
        reach_k = jnp.maximum(reach_k, square(got_ref[s, 64:128, :]))
        reach_q = jnp.maximum(reach_q, square(got_ref[s, 256:320, :]))
    v_scr[HEAD : 2 * HEAD, :] = jnp.ones((HEAD, DEVS * TOK), BF16)
    small = jnp.max(reach_k) * jnp.max(reach_q) <= BOUND * BOUND
    width = 512

    def query_of(i):
        return jnp.concatenate([got_ref[4 * i + j, 256:320, :] for j in range(4)], axis=1)

    def finish(i, acc):
        out = (acc[:HEAD] / acc[HEAD : HEAD + 1]).astype(BF16)
        for j in range(4):
            out_ref[4 * i + j] = out[:, j * 128 : (j + 1) * 128]

    @pl.when(small)
    def _():
        def tile(i, _):
            scores = jnp.dot(k_scr[...], query_of(i), preferred_element_type=F32)
            weights = jnp.exp2(scores).astype(BF16)
            finish(i, jnp.dot(v_scr[...], weights, preferred_element_type=F32))
            return 0

        lax.fori_loop(0, 8, tile, 0)

    @pl.when(jnp.logical_not(small))
    def _():
        chunk = 256

        def tile(i, _):
            query = query_of(i)

            def one(c, carry):
                acc, top = carry
                off = pl.multiple_of(c * chunk, chunk)
                scores = jnp.dot(k_scr[pl.ds(off, chunk), :], query, preferred_element_type=F32)
                new_top = jnp.maximum(top, jnp.max(scores, axis=0, keepdims=True))
                weights = jnp.exp2(scores - new_top).astype(BF16)
                acc = acc * jnp.exp2(top - new_top) + jnp.dot(
                    v_scr[0 : HEAD + 16, pl.ds(off, chunk)], weights, preferred_element_type=F32
                )
                return acc, new_top

            begin = (jnp.zeros((HEAD + 16, width), F32), jnp.full((1, width), -3e38, F32))
            acc, _ = lax.fori_loop(0, DEVS * TOK // chunk, one, begin)
            finish(i, acc)
            return 0

        lax.fori_loop(0, 8, tile, 0)


def back_kernel(
    att_ref, resid_ref, wout_ref, obias_ref, gain_ref, shift_ref, fc1_ref, b1_ref, fc2_ref,
    b2_ref, out_ref,
):
    mixed = jnp.concatenate(
        [
            lax.dot_general(
                att_ref[g * HEADS : (g + 1) * HEADS].reshape(D, 128),
                wout_ref[...],
                (((0,), (0,)), ((), ())),
                preferred_element_type=F32,
            )
            for g in range(2)
        ],
        axis=0,
    )
    stream = (resid_ref[...].astype(F32) + mixed + obias_ref[...]).astype(BF16)
    wide = stream.astype(F32)
    normed = layer_norm(wide, gain_ref[...], shift_ref[...]).astype(BF16)
    acc = wide + b2_ref[...]
    chunk = 1024
    for f in range(0, FF, chunk):
        pre = jnp.dot(normed, fc1_ref[:, f : f + chunk], preferred_element_type=F32)
        pre = pre + b1_ref[:, f : f + chunk]
        hidden = (0.5 * pre * (1.0 + lax.erf(pre * math.sqrt(0.5)))).astype(BF16)
        acc = acc + jnp.dot(hidden, fc2_ref[f : f + chunk, :], preferred_element_type=F32)
    out_ref[...] = acc.astype(BF16)


def call_whole(kernel, operands, out_shape, name, limit, scratch=(), smem=(), hbm=()):
    def space(i):
        return pltpu.SMEM if i in smem else pl.ANY if i in hbm else pltpu.VMEM

    specs = [pl.BlockSpec(memory_space=space(i)) for i in range(len(operands))]
    many = isinstance(out_shape, (list, tuple))
    out_specs = pl.BlockSpec(memory_space=pltpu.VMEM)
    return pl.pallas_call(
        kernel,
        in_specs=specs,
        out_specs=[out_specs] * len(out_shape) if many else out_specs,
        out_shape=out_shape,
        scratch_shapes=list(scratch),
        compiler_params=pltpu.CompilerParams(vmem_limit_bytes=limit * 2**20),
        name=name,
    )(*operands)


def per_device(
    density, stem_weight, stem_bias, pos_embed, ln1_gain, ln1_bias, w_qkv, qkv_bias, w_out,
    out_bias, ln2_gain, ln2_bias, w_fc1, fc1_bias, w_fc2, fc2_bias,
):
    row = lambda v: v.reshape(1, -1)
    shape = jax.ShapeDtypeStruct
    everyone = lambda v: lax.all_to_all(v, "ctx", split_axis=0, concat_axis=0, tiled=True)
    index = lax.axis_index("ctx").astype(jnp.int32).reshape(1)
    first = call_whole(
        start_kernel, (index, density), shape((DEVS, 40, 128), F32), "start", 4, smem=(0,)
    )
    got = everyone(first)
    send, residual = call_whole(
        front_kernel,
        (index, got, density, stem_weight, row(stem_bias), pos_embed, row(ln1_gain),
         row(ln1_bias), row(qkv_bias), w_qkv),
        [shape((DEVS, 320, 128), BF16), shape((TOK, D), BF16)],
        "front",
        20,
        scratch=(
            pltpu.VMEM((SIDE, 80, 128), F32),
            pltpu.VMEM((384, 2048), BF16),
            pltpu.VMEM((6, D, 512), BF16),
            pltpu.SemaphoreType.DMA((6,)),
        ),
        smem=(0,),
        hbm=(9,),
    )
    mixed = call_whole(
        attend_kernel,
        (everyone(send),),
        shape((DEVS, HEAD, 128), BF16),
        "attend",
        20,
        scratch=(
            pltpu.VMEM((DEVS * TOK, HEAD), BF16),
            pltpu.VMEM((2 * HEAD, DEVS * TOK), BF16),
        ),
    )
    return call_whole(
        back_kernel,
        (everyone(mixed), residual, w_out, row(out_bias), row(ln2_gain), row(ln2_bias),
         w_fc1, row(fc1_bias), w_fc2, row(fc2_bias)),
        shape((TOK, D), BF16),
        "back",
        16,
    )


def solution(mesh):
    rest = [P()] * 12
    in_specs = (P(("dp", "ctx"), None, None), P(), P(), P("ctx", None), *rest)
    return jax.shard_map(
        per_device, mesh=mesh, in_specs=in_specs, out_specs=P(("dp", "ctx"), None), check_vma=False
    )
```

time: 206 us -> 212 us (1.029)
  Pallas kernels: 90.9 us -> 129 us
  starting transfers between devices: 15.6 us -> 0 us
  blocking collectives: 84.3 us -> 72.3 us
  waiting for transfers between devices: 4.14 us -> 0 us
  other arithmetic: 3.28 us -> 0.01 us
  local copies, waits for them, and re-layouts: 6.49 us -> 9.46 us
    pallas_call x2 -> x4, Pallas kernels: 14 us -> 129 us  [call_whole(): pl.pallas_call(kernel, in_specs=specs, out_specs=[out_specs] * len(out_sh...]
    pallas_call x2 -> x0, Pallas kernels: 76.9 us -> none  [attend(): pl.pallas_call(functools.partial(attend_kernel, last=last), grid=(queries...]
    all_to_all x2 -> x3, blocking collectives: 84.3 us -> 72.3 us  [per_device(): lax.all_to_all(v, 'ctx', split_axis=0, concat_axis=0, tiled=True)]
    all_to_all x1 -> x0, starting transfers between devices: 8.83 us -> none  [per_device(): lax.all_to_all(jnp.broadcast_to(local, (32, 1, 1)), axis, split_axis=0, c...]
    ppermute x3 -> x0, starting transfers between devices: 6.78 us -> none  [the longest x1 4.55 us: per_device(): low = lax.ppermute(density[3:4], axis, up)]
    unnamed x30 -> x36, local copies, waits for them, and re-layouts: 2.85 us -> 9.46 us
    ppermute x3 -> x0, waiting for transfers between devices: 4.14 us -> none  [the longest x1 4.14 us: per_device(): lax.ppermute(got[:, :2 * HEAD, :], axis, [(i, i ^ PLANE) for i in range(3...]
  transfers between devices with their start and end apart: 4 -> 0, of which waited for: 1 -> 0; matrix products, arithmetic and copies ran while one was open for 2% -> 0% of each run, Pallas kernels for 9% -> 0%
where the time goes in v1:
time: 212 us; the launch traced here: 211 us
  Pallas kernels  129 us (61%)
  blocking collectives  72.3 us (34%)
  local copies, waits for them, and re-layouts  9.46 us (4%)
    pallas_call x4, Pallas kernels, call_whole(): pl.pallas_call(kernel, in_specs=specs, out_specs=[out_specs] * len(out_sh...  129 us
    all_to_all x3, blocking collectives, per_device(): lax.all_to_all(v, 'ctx', split_axis=0, concat_axis=0, tiled=True)  72.3 us
    unnamed x36, local copies, waits for them, and re-layouts  9.46 us

profile of v1, /device:TPU:0, one launch (start us, length us, event | category | flops | bytes accessed | tf_op | source)
XLA Modules:
  0.0 211.1 jit_solution(8699695451017664937)
XLA Ops:
  0.0 0.0 copy-start.3
  0.0 0.9 copy-done.3
  0.9 0.2 start.1
  1.1 21.3 %all_to_all.15.got_ref = f32[32,40,128]{2,1,0:T(8,128)S(1)} all-to-all(f32[32,40,128]{2,1,0:T(8,128)S(1)} %start.1), channel_id=1, replica_groups=mesh['dp'=4,'ctx'=32] {'ctx'}, dimensions={0} | all-to-all | bytes 1310720 | tf_op jit(solution)/shard_map/all_to_all | solution.py:242
  22.4 2.8 %copy-done.1 = bf16[1024,3072]{1,0:T(8,128)(2,1)S(1)} copy-done((bf16[1024,3072]{1,0:T(8,128)(2,1)S(1)}, bf16[1024,3072]{1,0:T(8,128)(2,1)}, u32[]{:S(2)}) %copy-start.1) | copy-done | bytes 6291480
  25.1 0.9 copy-done.4
  26.0 1.0 copy-done.5
  27.1 1.0 copy-done.6
  28.1 0.7 copy-done.8
  28.8 0.7 copy-done.9
  29.5 0.7 copy-done.10
  30.2 0.7 copy-done.11
  30.9 6.0 %front.1 = (bf16[32,320,128]{2,1,0:T(8,128)(2,1)S(1)}, bf16[256,1024]{1,0:T(8,128)(2,1)S(1)}) custom-call(s32[1]{0:T(128)} %bitcast.index_ref, f32[32,40,128]{2,1,0:T(8,128)S(1)} %all_to_all.15.got_ref, f32[4,64,64]{2,1,0:T(8,128)S(1)} %copy-done.4, bf16[216,1024]{1,0:T(8,128)(2,1)S(1)} %copy-done.6, f32[1,1024]{1,0:T(1,128)S(1)} %bitcast.14, ...), custom_call_target="tpu_custom_call" | custom-call | tf_op jit(solution)/shard_map/front/pallas_call | solution.py:225
  36.9 0.0 copy-start.7
  36.9 0.0 copy-start.12
  36.9 0.0 copy-start.13
  36.9 0.0 copy-start.14
  36.9 0.0 copy-start.15
  36.9 0.0 slice-start.1
  37.0 36.9 %all_to_all.16.got_ref = bf16[32,320,128]{2,1,0:T(8,128)(2,1)S(1)} all-to-all(bf16[32,320,128]{2,1,0:T(8,128)(2,1)S(1)} %get-tuple-element.7), channel_id=1, replica_groups=mesh['dp'=4,'ctx'=32] {'ctx'}, dimensions={0} | all-to-all | bytes 5242880 | tf_op jit(solution)/shard_map/all_to_all | solution.py:242
  73.8 116.7 %attend.1 = bf16[32,64,128]{2,1,0:T(8,128)(2,1)S(1)} custom-call(bf16[32,320,128]{2,1,0:T(8,128)(2,1)S(1)} %all_to_all.16.got_ref), custom_call_target="tpu_custom_call" | custom-call | tf_op jit(solution)/shard_map/attend/pallas_call | solution.py:225
  190.5 14.1 %all_to_all.17.att_ref = bf16[32,64,128]{2,1,0:T(8,128)(2,1)S(1)} all-to-all(bf16[32,64,128]{2,1,0:T(8,128)(2,1)S(1)} %attend.1), channel_id=1, replica_groups=mesh['dp'=4,'ctx'=32] {'ctx'}, dimensions={0} | all-to-all | bytes 1048576 | tf_op jit(solution)/shard_map/all_to_all | solution.py:242
  204.7 0.0 copy-done.2
  204.7 0.0 slice-done
  204.7 0.0 copy-done
  204.7 0.0 copy-done.7
  204.7 0.0 copy-done.12
  204.7 0.0 copy-done.13
  204.7 0.0 copy-done.14
  204.7 0.0 copy-done.15
  204.7 0.0 slice-done.1
  204.7 6.4 %back.1 = bf16[256,1024]{1,0:T(8,128)(2,1)} custom-call(bf16[32,64,128]{2,1,0:T(8,128)(2,1)S(1)} %all_to_all.17.att_ref, bf16[256,1024]{1,0:T(8,128)(2,1)S(1)} %get-tuple-element.8.resid_ref, bf16[1024,1024]{1,0:T(8,128)(2,1)S(1)} %copy-done.2, f32[1,1024]{1,0:T(1,128)S(1)} %bitcast.17, f32[1,1024]{1,0:T(1,128)S(1)} %bitcast.18, f32[1,1024]{1,0:T(1,128)S(1)} %bitcast.19, ...), custom_call_target="tpu_custom_call" | custom-call | tf_op jit(solution)/shard_map/back/pallas_call | solution.py:225
  (12 shorter events, 0.0 us)
Async XLA Ops:
  0.0 0.9 copy-start.3
  0.9 203.7 %copy-start.2 = (bf16[1024,1024]{1,0:T(8,128)(2,1)S(1)}, bf16[1024,1024]{1,0:T(8,128)(2,1)}, u32[]{:S(2)}) copy-start(bf16[1024,1024]{1,0:T(8,128)(2,1)} %wout_ref.1) | copy-start | bytes 6291460
  22.4 2.8 %copy-start.1 = (bf16[1024,3072]{1,0:T(8,128)(2,1)S(1)}, bf16[1024,3072]{1,0:T(8,128)(2,1)}, u32[]{:S(2)}) copy-start(bf16[1024,3072]{1,0:T(8,128)(2,1)} %wqkv_hbm.1) | copy-start | bytes 18874372
  25.1 0.9 copy-start.4
  26.0 1.0 copy-start.5
  27.1 1.0 copy-start.6
  28.1 0.7 copy-start.8
  28.8 0.7 copy-start.9
  29.5 0.7 copy-start.10
  30.2 0.7 copy-start.11
  30.9 173.8 %slice-start = ((s8[8388608]{0:T(1024)(128)(4,1)}), s8[4194304]{0:T(1024)(128)(4,1)S(1)}, s32[]{:S(2)}) async-start(s8[8388608]{0:T(1024)(128)(4,1)} %bitcast.10), calls=%async_computation.3 | async-start | bytes 8388608
  30.9 173.8 %copy-start = (bf16[4096,1024]{1,0:T(8,128)(2,1)S(1)}, bf16[4096,1024]{1,0:T(8,128)(2,1)}, u32[]{:S(2)}) copy-start(bf16[4096,1024]{1,0:T(8,128)(2,1)} %fc2_ref.1) | copy-start | bytes 25165828
  36.9 167.8 %copy-start.7 = (f32[4096]{0:T(1024)S(1)}, f32[4096]{0:T(1024)}, u32[]{:S(2)}) copy-start(f32[4096]{0:T(1024)} %param.29) | copy-start | bytes 49156
  36.9 167.8 %copy-start.12 = (f32[1024]{0:T(1024)S(1)}, f32[1024]{0:T(1024)}, u32[]{:S(2)}) copy-start(f32[1024]{0:T(1024)} %param.25) | copy-start | bytes 12292
  36.9 167.8 %copy-start.13 = (f32[1024]{0:T(1024)S(1)}, f32[1024]{0:T(1024)}, u32[]{:S(2)}) copy-start(f32[1024]{0:T(1024)} %param.26) | copy-start | bytes 12292
  36.9 167.8 %copy-start.14 = (f32[1024]{0:T(1024)S(1)}, f32[1024]{0:T(1024)}, u32[]{:S(2)}) copy-start(f32[1024]{0:T(1024)} %param.27) | copy-start | bytes 12292
  36.9 167.8 %copy-start.15 = (f32[1024]{0:T(1024)S(1)}, f32[1024]{0:T(1024)}, u32[]{:S(2)}) copy-start(f32[1024]{0:T(1024)} %param.31) | copy-start | bytes 12292
  36.9 167.8 %slice-start.1 = ((s8[8388608]{0:T(1024)(128)(4,1)}), s8[4194304]{0:T(1024)(128)(4,1)S(1)}, s32[]{:S(2)}) async-start(s8[8388608]{0:T(1024)(128)(4,1)} %bitcast.10), calls=%async_computation.4 | async-start | bytes 8388608

commit v2 on v1

--- a/solution.py
+++ b/solution.py
@@ -44,16 +44,8 @@
 
 def front_kernel(
     index_ref, got_ref, mid_ref, stem_ref, sbias_ref, pos_ref, gain_ref, shift_ref, qbias_ref,
-    wqkv_hbm, send_ref, resid_ref, cols_ref, pick_ref, wqkv_ref, sems,
-):
-    copies = [
-        pltpu.make_async_copy(
-            wqkv_hbm.at[:, pl.ds(n * 512, 512)], wqkv_ref.at[n], sems.at[n]
-        )
-        for n in range(6)
-    ]
-    for copy in copies:
-        copy.start()
+    wqkv_ref, send_ref, resid_ref, cols_ref, pick_ref,
+):
     index = index_ref[0]
     row = lax.broadcasted_iota(jnp.int32, (64, 2048), 0)
     col = lax.broadcasted_iota(jnp.int32, (64, 2048), 1)
@@ -100,8 +92,7 @@
     for part in range(3):
         for n in range(2):
             start = part * D + n * 512
-            copies[part * 2 + n].wait()
-            out = jnp.dot(normed, wqkv_ref[part * 2 + n], preferred_element_type=F32)
+            out = jnp.dot(normed, wqkv_ref[:, start : start + 512], preferred_element_type=F32)
             out = out + qbias_ref[:, start : start + 512]
             if part == 0:
                 out = out * scale
@@ -122,7 +113,13 @@
                             send_ref[head + g * HEADS, base + 64 : base + 128, :] = right
 
 
-def attend_kernel(got_ref, out_ref, k_scr, v_scr):
+def attend_kernel(
+    got_ref, wout_hbm, fc1_hbm, fc2_hbm, out_ref, wout_ref, fc1_ref, fc2_ref, k_scr, v_scr, sems,
+):
+    pairs = ((wout_hbm, wout_ref), (fc1_hbm, fc1_ref), (fc2_hbm, fc2_ref))
+    copies = [pltpu.make_async_copy(a, b, sems.at[n]) for n, (a, b) in enumerate(pairs)]
+    for copy in copies:
+        copy.start()
     zero = jnp.zeros((1, 128), F32)
     reach_k, reach_q = zero, zero
 
@@ -185,6 +182,9 @@
 
         lax.fori_loop(0, 8, tile, 0)
 
+    for copy in copies:
+        copy.wait()
+
 
 def back_kernel(
     att_ref, resid_ref, wout_ref, obias_ref, gain_ref, shift_ref, fc1_ref, b1_ref, fc2_ref,
@@ -215,9 +215,9 @@
     out_ref[...] = acc.astype(BF16)
 
 
-def call_whole(kernel, operands, out_shape, name, limit, scratch=(), smem=(), hbm=()):
+def call_whole(kernel, operands, out_shape, name, limit, scratch=(), smem=(), hbm=(), giga=1):
     def space(i):
-        return pltpu.SMEM if i in smem else pl.ANY if i in hbm else pltpu.VMEM
+        return pltpu.SMEM if i in smem else pltpu.HBM if i in hbm else pltpu.VMEM
 
     specs = [pl.BlockSpec(memory_space=space(i)) for i in range(len(operands))]
     many = isinstance(out_shape, (list, tuple))
@@ -229,6 +229,9 @@
         out_shape=out_shape,
         scratch_shapes=list(scratch),
         compiler_params=pltpu.CompilerParams(vmem_limit_bytes=limit * 2**20),
+        cost_estimate=pl.CostEstimate(
+            flops=giga * 10**9, bytes_accessed=10**6, transcendentals=0
+        ),
         name=name,
     )(*operands)
 
@@ -242,7 +245,8 @@
     everyone = lambda v: lax.all_to_all(v, "ctx", split_axis=0, concat_axis=0, tiled=True)
     index = lax.axis_index("ctx").astype(jnp.int32).reshape(1)
     first = call_whole(
-        start_kernel, (index, density), shape((DEVS, 40, 128), F32), "start", 4, smem=(0,)
+        start_kernel, (index, density), shape((DEVS, 40, 128), F32), "start", 4, smem=(0,),
+        giga=20,
     )
     got = everyone(first)
     send, residual = call_whole(
@@ -255,22 +259,27 @@
         scratch=(
             pltpu.VMEM((SIDE, 80, 128), F32),
             pltpu.VMEM((384, 2048), BF16),
-            pltpu.VMEM((6, D, 512), BF16),
-            pltpu.SemaphoreType.DMA((6,)),
         ),
         smem=(0,),
-        hbm=(9,),
-    )
-    mixed = call_whole(
+    )
+    mixed, w_out, w_fc1, w_fc2 = call_whole(
         attend_kernel,
-        (everyone(send),),
-        shape((DEVS, HEAD, 128), BF16),
+        (everyone(send), w_out, w_fc1, w_fc2),
+        [
+            shape((DEVS, HEAD, 128), BF16),
+            shape(w_out.shape, BF16),
+            shape(w_fc1.shape, BF16),
+            shape(w_fc2.shape, BF16),
+        ],
         "attend",
-        20,
+        24,
         scratch=(
             pltpu.VMEM((DEVS * TOK, HEAD), BF16),
             pltpu.VMEM((2 * HEAD, DEVS * TOK), BF16),
+            pltpu.SemaphoreType.DMA((3,)),
         ),
+        hbm=(1, 2, 3),
+        giga=28,
     )
     return call_whole(
         back_kernel,

time: 212 us -> 200 us (0.943)
  local copies, waits for them, and re-layouts: 9.46 us -> 0.96 us
    unnamed x36 -> x28, local copies, waits for them, and re-layouts: 9.46 us -> 0.96 us
where the time goes in v2:
time: 200 us
  Pallas kernels  127 us (64%)
  blocking collectives  71.7 us (36%)
    pallas_call x4, Pallas kernels, call_whole(): pl.pallas_call(kernel, in_specs=specs, out_specs=[out_specs] * len(out_sh...  127 us
    all_to_all x3, blocking collectives, per_device(): lax.all_to_all(v, 'ctx', split_axis=0, concat_axis=0, tiled=True)  71.7 us

profile of v2, /device:TPU:0, one launch (start us, length us, event | category | flops | bytes accessed | tf_op | source)
XLA Modules:
  0.0 200.0 jit_solution(1819299344476472643)
XLA Ops:
  0.0 0.0 copy-start.3
  0.0 0.9 copy-done.3
  0.9 0.0 copy-start
  0.9 0.0 copy-start.1
  0.9 0.0 copy-start.2
  0.9 0.0 copy-start.5
  0.9 0.0 copy-start.6
  0.9 0.0 copy-start.7
  0.9 0.0 copy-start.8
  0.9 0.2 start.1
  1.1 21.4 %all_to_all.15.got_ref = f32[32,40,128]{2,1,0:T(8,128)S(1)} all-to-all(f32[32,40,128]{2,1,0:T(8,128)S(1)} %start.1), channel_id=1, replica_groups=mesh['dp'=4,'ctx'=32] {'ctx'}, dimensions={0} | all-to-all | bytes 1310720 | tf_op jit(solution)/shard_map/all_to_all | solution.py:245
  22.5 0.0 copy-done
  22.5 0.0 copy-done.1
  22.5 0.0 copy-done.2
  22.5 0.0 copy-done.5
  22.6 0.0 copy-done.6
  22.6 0.0 copy-done.7
  22.6 0.0 copy-done.8
  22.6 0.0 copy-start.13
  22.6 3.7 %front.1 = (bf16[32,320,128]{2,1,0:T(8,128)(2,1)S(1)}, bf16[256,1024]{1,0:T(8,128)(2,1)S(1)}) custom-call(s32[1]{0:T(128)} %bitcast.index_ref, f32[32,40,128]{2,1,0:T(8,128)S(1)} %all_to_all.15.got_ref, f32[4,64,64]{2,1,0:T(8,128)S(1)} %copy-done.3, bf16[216,1024]{1,0:T(8,128)(2,1)S(1)} %copy-done.2, f32[1,1024]{1,0:T(1,128)S(1)} %bitcast.12, ...), custom_call_target="tpu_custom_call" | custom-call | flops 1000000000 | bytes 1000000 | tf_op jit(solution)/shard_map/front/pallas_call | solution.py:225
  26.3 36.6 %all_to_all.16.got_ref = bf16[32,320,128]{2,1,0:T(8,128)(2,1)S(1)} all-to-all(bf16[32,320,128]{2,1,0:T(8,128)(2,1)S(1)} %get-tuple-element.11), channel_id=1, replica_groups=mesh['dp'=4,'ctx'=32] {'ctx'}, dimensions={0} | all-to-all | bytes 5242880 | tf_op jit(solution)/shard_map/all_to_all | solution.py:245
  62.9 0.0 copy-done.13
  62.9 0.0 copy-start.11
  62.9 0.0 copy-start.12
  62.9 116.9 %attend.1 = (bf16[32,64,128]{2,1,0:T(8,128)(2,1)S(1)}, bf16[1024,1024]{1,0:T(8,128)(2,1)S(1)}, bf16[1024,4096]{1,0:T(8,128)(2,1)S(1)}, bf16[4096,1024]{1,0:T(8,128)(2,1)S(1)}) custom-call(bf16[32,320,128]{2,1,0:T(8,128)(2,1)S(1)} %all_to_all.16.got_ref, bf16[1024,1024]{1,0:T(8,128)(2,1)S(1)} %copy-done.13, bf16[1024,4096]{1,0:T(8,128)(2,1)} %fc1_hbm.1, ...), custom_call_target="tpu_custom_call" | custom-call | flops 28000000000 | bytes 1000000 | tf_op jit(solution)/shard_map/attend/pallas_call | solution.py:225
  179.8 13.7 %all_to_all.17.att_ref = bf16[32,64,128]{2,1,0:T(8,128)(2,1)S(1)} all-to-all(bf16[32,64,128]{2,1,0:T(8,128)(2,1)S(1)} %get-tuple-element.12), channel_id=1, replica_groups=mesh['dp'=4,'ctx'=32] {'ctx'}, dimensions={0} | all-to-all | bytes 1048576 | tf_op jit(solution)/shard_map/all_to_all | solution.py:245
  193.6 0.0 copy-done.4
  193.6 0.0 copy-done.9
  193.6 0.0 copy-done.10
  193.6 0.0 copy-done.11
  193.6 0.0 copy-done.12
  193.6 6.4 %back.1 = bf16[256,1024]{1,0:T(8,128)(2,1)} custom-call(bf16[32,64,128]{2,1,0:T(8,128)(2,1)S(1)} %all_to_all.17.att_ref, bf16[256,1024]{1,0:T(8,128)(2,1)S(1)} %get-tuple-element.13.resid_ref, bf16[1024,1024]{1,0:T(8,128)(2,1)S(1)} %get-tuple-element.14.wout_ref, f32[1,1024]{1,0:T(1,128)S(1)} %bitcast.15, f32[1,1024]{1,0:T(1,128)S(1)} %bitcast.16, ...), custom_call_target="tpu_custom_call" | custom-call | flops 1000000000 | bytes 1000000 | tf_op jit(solution)/shard_map/back/pallas_call | solution.py:225
  (3 shorter events, 0.0 us)
Async XLA Ops:
  0.0 0.9 copy-start.3
  0.9 21.6 %copy-start = (bf16[1024,3072]{1,0:T(8,128)(2,1)S(1)}, bf16[1024,3072]{1,0:T(8,128)(2,1)}, u32[]{:S(2)}) copy-start(bf16[1024,3072]{1,0:T(8,128)(2,1)} %wqkv_ref.1) | copy-start | bytes 18874372
  0.9 21.6 %copy-start.1 = (bf16[256,1024]{1,0:T(8,128)(2,1)S(1)}, bf16[256,1024]{1,0:T(8,128)(2,1)}, u32[]{:S(2)}) copy-start(bf16[256,1024]{1,0:T(8,128)(2,1)} %pos_ref.1) | copy-start | bytes 1572868
  0.9 21.6 %copy-start.2 = (bf16[216,1024]{1,0:T(8,128)(2,1)S(1)}, bf16[216,1024]{1,0:T(8,128)(2,1)}, u32[]{:S(2)}) copy-start(bf16[216,1024]{1,0:T(8,128)(2,1)} %stem_ref.1) | copy-start | bytes 1327108
  0.9 21.6 %copy-start.5 = (f32[3072]{0:T(1024)S(1)}, f32[3072]{0:T(1024)}, u32[]{:S(2)}) copy-start(f32[3072]{0:T(1024)} %param.23) | copy-start | bytes 36868
  0.9 21.6 %copy-start.6 = (f32[1024]{0:T(1024)S(1)}, f32[1024]{0:T(1024)}, u32[]{:S(2)}) copy-start(f32[1024]{0:T(1024)} %param.18) | copy-start | bytes 12292
  0.9 21.6 %copy-start.7 = (f32[1024]{0:T(1024)S(1)}, f32[1024]{0:T(1024)}, u32[]{:S(2)}) copy-start(f32[1024]{0:T(1024)} %param.20) | copy-start | bytes 12292
  0.9 21.6 %copy-start.8 = (f32[1024]{0:T(1024)S(1)}, f32[1024]{0:T(1024)}, u32[]{:S(2)}) copy-start(f32[1024]{0:T(1024)} %param.21) | copy-start | bytes 12292
  22.6 40.3 %copy-start.13 = (bf16[1024,1024]{1,0:T(8,128)(2,1)S(1)}, bf16[1024,1024]{1,0:T(8,128)(2,1)}, u32[]{:S(2)}) copy-start(bf16[1024,1024]{1,0:T(8,128)(2,1)} %wout_hbm.1) | copy-start | bytes 6291460
  62.9 130.7 %copy-start.4 = (f32[4096]{0:T(1024)S(1)}, f32[4096]{0:T(1024)}, u32[]{:S(2)}) copy-start(f32[4096]{0:T(1024)} %param.29) | copy-start | bytes 49156
  62.9 130.7 %copy-start.9 = (f32[1024]{0:T(1024)S(1)}, f32[1024]{0:T(1024)}, u32[]{:S(2)}) copy-start(f32[1024]{0:T(1024)} %param.25) | copy-start | bytes 12292
  62.9 130.7 %copy-start.10 = (f32[1024]{0:T(1024)S(1)}, f32[1024]{0:T(1024)}, u32[]{:S(2)}) copy-start(f32[1024]{0:T(1024)} %param.26) | copy-start | bytes 12292
  62.9 130.7 %copy-start.11 = (f32[1024]{0:T(1024)S(1)}, f32[1024]{0:T(1024)}, u32[]{:S(2)}) copy-start(f32[1024]{0:T(1024)} %param.27) | copy-start | bytes 12292
  62.9 130.7 %copy-start.12 = (f32[1024]{0:T(1024)S(1)}, f32[1024]{0:T(1024)}, u32[]{:S(2)}) copy-start(f32[1024]{0:T(1024)} %param.31) | copy-start | bytes 12292

commit v3 on v2

--- a/solution.py
+++ b/solution.py
@@ -14,6 +14,7 @@
 SIDE = 16
 TOK = 256
 DEVS = 32
+VOXELS = 4 * 64 * 64
 BOUND = 100.0
 F32 = jnp.float32
 BF16 = jnp.bfloat16
@@ -27,15 +28,25 @@
 
 def start_kernel(index_ref, density_ref, out_ref):
     index = index_ref[0]
-    total = jnp.sum(density_ref[...]) * jnp.ones((8, 128), F32)
+    total = jnp.sum(density_ref[...]) * jnp.ones((16, 128), F32)
+    local = total[0:1, :64] / VOXELS
+    high = total.astype(BF16)
+    left = total - high.astype(F32)
+    middle = left.astype(BF16)
+    low = (left - middle.astype(F32)).astype(BF16)
+    row = lax.broadcasted_iota(jnp.int32, (16, 128), 0)
+    pieces = jnp.where(row == 0, high.astype(F32), 0.0)
+    pieces = jnp.where(row == 1, middle.astype(F32), pieces)
+    pieces = jnp.where(row == 2, low.astype(F32), pieces).astype(BF16)
 
     def packed(plane):
-        return jnp.concatenate([plane[:32], plane[32:]], axis=1)
+        field = jnp.log(plane / local)
+        return jnp.concatenate([field[:32], field[32:]], axis=1).astype(BF16)
 
     bottom = packed(density_ref[0])
     for d in range(DEVS):
         out_ref[d, 0:32, :] = bottom
-        out_ref[d, 32:40, :] = total
+        out_ref[d, 32:48, :] = pieces
 
     @pl.when(index < DEVS - 1)
     def _():
@@ -59,18 +70,20 @@
     order = jnp.where((row % 48 < 36) & (col == (row % 48) * 6 + row // 48), 1.0, 0.0)
     stem = jnp.dot(order.astype(BF16), stem_ref[...], preferred_element_type=F32).astype(BF16)
 
-    total = jnp.sum(got_ref[:, 32:33, :], axis=0)
-    mean = total[:, 0:64] / (DEVS * 4 * 64 * 64)
+    sums = jnp.sum(got_ref[:, 32:48, :].astype(F32), axis=1)
+    mean = jnp.sum(sums, axis=0, keepdims=True)[:, :64] / (DEVS * VOXELS)
 
     def halo(source, valid):
-        block = got_ref[source, 0:32, :]
+        block = got_ref[source, 0:32, :].astype(F32)
         plane = jnp.concatenate([block[:, :64], block[:, 64:]], axis=0)
-        return jnp.where(valid, plane, mean)
+        local = jnp.sum(got_ref[source, 32:48, :].astype(F32), axis=0, keepdims=True)
+        shift = jnp.log(local[:, :64] / VOXELS / mean)
+        return jnp.where(valid, plane + shift, 0.0).astype(BF16)
 
     low = halo(jnp.maximum(index - 1, 0), index > 0)
     high = halo(jnp.minimum(index + 1, DEVS - 1), index < DEVS - 1)
-    planes = [low] + [mid_ref[a] for a in range(4)] + [high]
-    field = jnp.concatenate([jnp.log(p / mean).astype(BF16) for p in planes], axis=0)
+    planes = [low] + [jnp.log(mid_ref[a] / mean).astype(BF16) for a in range(4)] + [high]
+    field = jnp.concatenate(planes, axis=0)
     cols_ref[:, 0:8, :] = jnp.zeros((SIDE, 8, 128), F32)
     cols_ref[:, 72:80, :] = jnp.zeros((SIDE, 8, 128), F32)
     picked = lax.dot_general(
@@ -245,7 +258,7 @@
     everyone = lambda v: lax.all_to_all(v, "ctx", split_axis=0, concat_axis=0, tiled=True)
     index = lax.axis_index("ctx").astype(jnp.int32).reshape(1)
     first = call_whole(
-        start_kernel, (index, density), shape((DEVS, 40, 128), F32), "start", 4, smem=(0,),
+        start_kernel, (index, density), shape((DEVS, 48, 128), BF16), "start", 4, smem=(0,),
         giga=20,
     )
     got = everyone(first)

time: 200 us -> 198 us (0.990)
  blocking collectives: 71.7 us -> 69 us
    all_to_all x3, blocking collectives: 71.7 us -> 69 us  [per_device(): lax.all_to_all(v, 'ctx', split_axis=0, concat_axis=0, tiled=True)]
where the time goes in v3:
time: 198 us; the launch traced here: 197 us
  Pallas kernels  127 us (64%)
  blocking collectives  69 us (35%)
    pallas_call x4, Pallas kernels, call_whole(): pl.pallas_call(kernel, in_specs=specs, out_specs=[out_specs] * len(out_sh...  127 us
    all_to_all x3, blocking collectives, per_device(): lax.all_to_all(v, 'ctx', split_axis=0, concat_axis=0, tiled=True)  69 us

profile of v3, /device:TPU:0, one launch (start us, length us, event | category | flops | bytes accessed | tf_op | source)
XLA Modules:
  0.0 197.3 jit_solution(12901640964427326458)
XLA Ops:
  0.0 0.0 copy-start.3
  0.0 0.9 copy-done.3
  0.9 0.0 copy-start
  0.9 0.0 copy-start.1
  0.9 0.0 copy-start.6
  0.9 0.0 copy-start.7
  0.9 0.0 copy-start.8
  0.9 0.0 copy-start.9
  1.0 0.3 start.1
  1.2 18.9 %all_to_all.15.got_ref = bf16[32,48,128]{2,1,0:T(8,128)(2,1)S(1)} all-to-all(bf16[32,48,128]{2,1,0:T(8,128)(2,1)S(1)} %start.1), channel_id=1, replica_groups=mesh['dp'=4,'ctx'=32] {'ctx'}, dimensions={0} | all-to-all | bytes 786432 | tf_op jit(solution)/shard_map/all_to_all | solution.py:258
  20.1 0.0 copy-done
  20.1 0.0 copy-done.1
  20.1 0.0 copy-done.2
  20.1 0.0 copy-done.4
  20.1 0.0 copy-done.6
  20.1 0.0 copy-done.7
  20.1 0.0 copy-done.8
  20.2 0.0 copy-done.9
  20.2 0.0 copy-start.14
  20.2 3.8 %front.1 = (bf16[32,320,128]{2,1,0:T(8,128)(2,1)S(1)}, bf16[256,1024]{1,0:T(8,128)(2,1)S(1)}) custom-call(s32[1]{0:T(128)} %bitcast.index_ref, bf16[32,48,128]{2,1,0:T(8,128)(2,1)S(1)} %all_to_all.15.got_ref, f32[4,64,64]{2,1,0:T(8,128)S(1)} %copy-done.4, bf16[216,1024]{1,0:T(8,128)(2,1)S(1)} %copy-done.2, f32[1,1024]{1,0:T(1,128)S(1)} %bitcast.12, ...), custom_call_target="tpu_custom_call" | custom-call | flops 1000000000 | bytes 1000000 | tf_op jit(solution)/shard_map/front/pallas_call | solution.py:238
  23.9 36.3 %all_to_all.16.got_ref = bf16[32,320,128]{2,1,0:T(8,128)(2,1)S(1)} all-to-all(bf16[32,320,128]{2,1,0:T(8,128)(2,1)S(1)} %get-tuple-element.11), channel_id=1, replica_groups=mesh['dp'=4,'ctx'=32] {'ctx'}, dimensions={0} | all-to-all | bytes 5242880 | tf_op jit(solution)/shard_map/all_to_all | solution.py:258
  60.3 0.0 copy-done.14
  60.3 0.0 copy-start.12
  60.3 0.0 copy-start.13
  60.3 116.9 %attend.1 = (bf16[32,64,128]{2,1,0:T(8,128)(2,1)S(1)}, bf16[1024,1024]{1,0:T(8,128)(2,1)S(1)}, bf16[1024,4096]{1,0:T(8,128)(2,1)S(1)}, bf16[4096,1024]{1,0:T(8,128)(2,1)S(1)}) custom-call(bf16[32,320,128]{2,1,0:T(8,128)(2,1)S(1)} %all_to_all.16.got_ref, bf16[1024,1024]{1,0:T(8,128)(2,1)S(1)} %copy-done.14, bf16[1024,4096]{1,0:T(8,128)(2,1)} %fc1_hbm.1, ...), custom_call_target="tpu_custom_call" | custom-call | flops 28000000000 | bytes 1000000 | tf_op jit(solution)/shard_map/attend/pallas_call | solution.py:238
  177.2 13.7 %all_to_all.17.att_ref = bf16[32,64,128]{2,1,0:T(8,128)(2,1)S(1)} all-to-all(bf16[32,64,128]{2,1,0:T(8,128)(2,1)S(1)} %get-tuple-element.12), channel_id=1, replica_groups=mesh['dp'=4,'ctx'=32] {'ctx'}, dimensions={0} | all-to-all | bytes 1048576 | tf_op jit(solution)/shard_map/all_to_all | solution.py:258
  190.9 0.0 copy-done.5
  190.9 0.0 copy-done.10
  190.9 0.0 copy-done.11
  190.9 0.0 copy-done.12
  191.0 0.0 copy-done.13
  191.0 6.4 %back.1 = bf16[256,1024]{1,0:T(8,128)(2,1)} custom-call(bf16[32,64,128]{2,1,0:T(8,128)(2,1)S(1)} %all_to_all.17.att_ref, bf16[256,1024]{1,0:T(8,128)(2,1)S(1)} %get-tuple-element.13.resid_ref, bf16[1024,1024]{1,0:T(8,128)(2,1)S(1)} %get-tuple-element.14.wout_ref, f32[1,1024]{1,0:T(1,128)S(1)} %bitcast.15, f32[1,1024]{1,0:T(1,128)S(1)} %bitcast.16, ...), custom_call_target="tpu_custom_call" | custom-call | flops 1000000000 | bytes 1000000 | tf_op jit(solution)/shard_map/back/pallas_call | solution.py:238
  (5 shorter events, 0.0 us)
Async XLA Ops:
  0.0 0.9 copy-start.3
  0.9 19.2 %copy-start = (bf16[1024,3072]{1,0:T(8,128)(2,1)S(1)}, bf16[1024,3072]{1,0:T(8,128)(2,1)}, u32[]{:S(2)}) copy-start(bf16[1024,3072]{1,0:T(8,128)(2,1)} %wqkv_ref.1) | copy-start | bytes 18874372
  0.9 19.2 %copy-start.1 = (bf16[256,1024]{1,0:T(8,128)(2,1)S(1)}, bf16[256,1024]{1,0:T(8,128)(2,1)}, u32[]{:S(2)}) copy-start(bf16[256,1024]{1,0:T(8,128)(2,1)} %pos_ref.1) | copy-start | bytes 1572868
  0.9 19.2 %copy-start.2 = (bf16[216,1024]{1,0:T(8,128)(2,1)S(1)}, bf16[216,1024]{1,0:T(8,128)(2,1)}, u32[]{:S(2)}) copy-start(bf16[216,1024]{1,0:T(8,128)(2,1)} %stem_ref.1) | copy-start | bytes 1327108
  0.9 19.2 %copy-start.4 = (f32[4,64,64]{2,1,0:T(8,128)S(1)}, f32[4,64,64]{2,1,0:T(8,128)}, u32[]{:S(2)}) copy-start(f32[4,64,64]{2,1,0:T(8,128)} %mid_ref.1) | copy-start | bytes 196612
  0.9 19.2 %copy-start.6 = (f32[3072]{0:T(1024)S(1)}, f32[3072]{0:T(1024)}, u32[]{:S(2)}) copy-start(f32[3072]{0:T(1024)} %param.23) | copy-start | bytes 36868
  0.9 19.2 %copy-start.7 = (f32[1024]{0:T(1024)S(1)}, f32[1024]{0:T(1024)}, u32[]{:S(2)}) copy-start(f32[1024]{0:T(1024)} %param.18) | copy-start | bytes 12292
  0.9 19.2 %copy-start.8 = (f32[1024]{0:T(1024)S(1)}, f32[1024]{0:T(1024)}, u32[]{:S(2)}) copy-start(f32[1024]{0:T(1024)} %param.20) | copy-start | bytes 12292
  0.9 19.2 %copy-start.9 = (f32[1024]{0:T(1024)S(1)}, f32[1024]{0:T(1024)}, u32[]{:S(2)}) copy-start(f32[1024]{0:T(1024)} %param.21) | copy-start | bytes 12292
  20.2 40.1 %copy-start.14 = (bf16[1024,1024]{1,0:T(8,128)(2,1)S(1)}, bf16[1024,1024]{1,0:T(8,128)(2,1)}, u32[]{:S(2)}) copy-start(bf16[1024,1024]{1,0:T(8,128)(2,1)} %wout_hbm.1) | copy-start | bytes 6291460
  60.3 130.7 %copy-start.5 = (f32[4096]{0:T(1024)S(1)}, f32[4096]{0:T(1024)}, u32[]{:S(2)}) copy-start(f32[4096]{0:T(1024)} %param.29) | copy-start | bytes 49156
  60.3 130.7 %copy-start.10 = (f32[1024]{0:T(1024)S(1)}, f32[1024]{0:T(1024)}, u32[]{:S(2)}) copy-start(f32[1024]{0:T(1024)} %param.25) | copy-start | bytes 12292
  60.3 130.7 %copy-start.11 = (f32[1024]{0:T(1024)S(1)}, f32[1024]{0:T(1024)}, u32[]{:S(2)}) copy-start(f32[1024]{0:T(1024)} %param.26) | copy-start | bytes 12292
  60.3 130.7 %copy-start.12 = (f32[1024]{0:T(1024)S(1)}, f32[1024]{0:T(1024)}, u32[]{:S(2)}) copy-start(f32[1024]{0:T(1024)} %param.27) | copy-start | bytes 12292
  60.3 130.7 %copy-start.13 = (f32[1024]{0:T(1024)S(1)}, f32[1024]{0:T(1024)}, u32[]{:S(2)}) copy-start(f32[1024]{0:T(1024)} %param.31) | copy-start | bytes 12292

commit v4 on v3

--- a/solution.py
+++ b/solution.py
@@ -28,13 +28,13 @@
 
 def start_kernel(index_ref, density_ref, out_ref):
     index = index_ref[0]
-    total = jnp.sum(density_ref[...]) * jnp.ones((16, 128), F32)
+    total = jnp.sum(density_ref[...]) * jnp.ones((8, 128), F32)
     local = total[0:1, :64] / VOXELS
     high = total.astype(BF16)
     left = total - high.astype(F32)
     middle = left.astype(BF16)
     low = (left - middle.astype(F32)).astype(BF16)
-    row = lax.broadcasted_iota(jnp.int32, (16, 128), 0)
+    row = lax.broadcasted_iota(jnp.int32, (8, 128), 0)
     pieces = jnp.where(row == 0, high.astype(F32), 0.0)
     pieces = jnp.where(row == 1, middle.astype(F32), pieces)
     pieces = jnp.where(row == 2, low.astype(F32), pieces).astype(BF16)
@@ -46,7 +46,7 @@
     bottom = packed(density_ref[0])
     for d in range(DEVS):
         out_ref[d, 0:32, :] = bottom
-        out_ref[d, 32:48, :] = pieces
+        out_ref[d, 32:40, :] = pieces
 
     @pl.when(index < DEVS - 1)
     def _():
@@ -70,13 +70,13 @@
     order = jnp.where((row % 48 < 36) & (col == (row % 48) * 6 + row // 48), 1.0, 0.0)
     stem = jnp.dot(order.astype(BF16), stem_ref[...], preferred_element_type=F32).astype(BF16)
 
-    sums = jnp.sum(got_ref[:, 32:48, :].astype(F32), axis=1)
+    sums = jnp.sum(got_ref[:, 32:40, :].astype(F32), axis=1)
     mean = jnp.sum(sums, axis=0, keepdims=True)[:, :64] / (DEVS * VOXELS)
 
     def halo(source, valid):
         block = got_ref[source, 0:32, :].astype(F32)
         plane = jnp.concatenate([block[:, :64], block[:, 64:]], axis=0)
-        local = jnp.sum(got_ref[source, 32:48, :].astype(F32), axis=0, keepdims=True)
+        local = jnp.sum(got_ref[source, 32:40, :].astype(F32), axis=0, keepdims=True)
         shift = jnp.log(local[:, :64] / VOXELS / mean)
         return jnp.where(valid, plane + shift, 0.0).astype(BF16)
 
@@ -258,7 +258,7 @@
     everyone = lambda v: lax.all_to_all(v, "ctx", split_axis=0, concat_axis=0, tiled=True)
     index = lax.axis_index("ctx").astype(jnp.int32).reshape(1)
     first = call_whole(
-        start_kernel, (index, density), shape((DEVS, 48, 128), BF16), "start", 4, smem=(0,),
+        start_kernel, (index, density), shape((DEVS, 40, 128), BF16), "start", 4, smem=(0,),
         giga=20,
     )
     got = everyone(first)

time: 198 us -> 197 us (level)
  no operation moved by 1% of the time
where the time goes in v4:
time: 197 us
  Pallas kernels  127 us (64%)
  blocking collectives  68.8 us (35%)
    pallas_call x4, Pallas kernels, call_whole(): pl.pallas_call(kernel, in_specs=specs, out_specs=[out_specs] * len(out_sh...  127 us
    all_to_all x3, blocking collectives, per_device(): lax.all_to_all(v, 'ctx', split_axis=0, concat_axis=0, tiled=True)  68.8 us

profile of v4, /device:TPU:0, one launch (start us, length us, event | category | flops | bytes accessed | tf_op | source)
XLA Modules:
  0.0 197.1 jit_solution(2568254358785815946)
XLA Ops:
  0.0 0.0 copy-start.3
  0.0 0.9 copy-done.3
  0.9 0.0 copy-start
  0.9 0.0 copy-start.2
  0.9 0.0 copy-start.6
  0.9 0.0 copy-start.7
  0.9 0.0 copy-start.8
  0.9 0.0 copy-start.9
  1.0 0.3 start.1
  1.2 18.3 %all_to_all.15.got_ref = bf16[32,40,128]{2,1,0:T(8,128)(2,1)S(1)} all-to-all(bf16[32,40,128]{2,1,0:T(8,128)(2,1)S(1)} %start.1), channel_id=1, replica_groups=mesh['dp'=4,'ctx'=32] {'ctx'}, dimensions={0} | all-to-all | bytes 655360 | tf_op jit(solution)/shard_map/all_to_all | solution.py:258
  19.5 0.0 copy-done
  19.5 0.0 copy-done.1
  19.5 0.0 copy-done.2
  19.5 0.0 copy-done.4
  19.6 0.0 copy-done.6
  19.6 0.0 copy-done.7
  19.6 0.0 copy-done.8
  19.6 0.0 copy-done.9
  19.6 0.0 copy-start.14
  19.6 3.8 %front.1 = (bf16[32,320,128]{2,1,0:T(8,128)(2,1)S(1)}, bf16[256,1024]{1,0:T(8,128)(2,1)S(1)}) custom-call(s32[1]{0:T(128)} %bitcast.index_ref, bf16[32,40,128]{2,1,0:T(8,128)(2,1)S(1)} %all_to_all.15.got_ref, f32[4,64,64]{2,1,0:T(8,128)S(1)} %copy-done.4, bf16[216,1024]{1,0:T(8,128)(2,1)S(1)} %copy-done.2, f32[1,1024]{1,0:T(1,128)S(1)} %bitcast.12, ...), custom_call_target="tpu_custom_call" | custom-call | flops 1000000000 | bytes 1000000 | tf_op jit(solution)/shard_map/front/pallas_call | solution.py:238
  23.4 36.3 %all_to_all.16.got_ref = bf16[32,320,128]{2,1,0:T(8,128)(2,1)S(1)} all-to-all(bf16[32,320,128]{2,1,0:T(8,128)(2,1)S(1)} %get-tuple-element.11), channel_id=1, replica_groups=mesh['dp'=4,'ctx'=32] {'ctx'}, dimensions={0} | all-to-all | bytes 5242880 | tf_op jit(solution)/shard_map/all_to_all | solution.py:258
  59.7 0.0 copy-done.14
  59.7 0.0 copy-start.12
  59.7 0.0 copy-start.13
  59.7 116.9 %attend.1 = (bf16[32,64,128]{2,1,0:T(8,128)(2,1)S(1)}, bf16[1024,1024]{1,0:T(8,128)(2,1)S(1)}, bf16[1024,4096]{1,0:T(8,128)(2,1)S(1)}, bf16[4096,1024]{1,0:T(8,128)(2,1)S(1)}) custom-call(bf16[32,320,128]{2,1,0:T(8,128)(2,1)S(1)} %all_to_all.16.got_ref, bf16[1024,1024]{1,0:T(8,128)(2,1)S(1)} %copy-done.14, bf16[1024,4096]{1,0:T(8,128)(2,1)} %fc1_hbm.1, ...), custom_call_target="tpu_custom_call" | custom-call | flops 28000000000 | bytes 1000000 | tf_op jit(solution)/shard_map/attend/pallas_call | solution.py:238
  176.6 14.1 %all_to_all.17.att_ref = bf16[32,64,128]{2,1,0:T(8,128)(2,1)S(1)} all-to-all(bf16[32,64,128]{2,1,0:T(8,128)(2,1)S(1)} %get-tuple-element.12), channel_id=1, replica_groups=mesh['dp'=4,'ctx'=32] {'ctx'}, dimensions={0} | all-to-all | bytes 1048576 | tf_op jit(solution)/shard_map/all_to_all | solution.py:258
  190.7 0.0 copy-done.5
  190.7 0.0 copy-done.10
  190.7 0.0 copy-done.11
  190.8 0.0 copy-done.12
  190.8 0.0 copy-done.13
  190.8 6.4 %back.1 = bf16[256,1024]{1,0:T(8,128)(2,1)} custom-call(bf16[32,64,128]{2,1,0:T(8,128)(2,1)S(1)} %all_to_all.17.att_ref, bf16[256,1024]{1,0:T(8,128)(2,1)S(1)} %get-tuple-element.13.resid_ref, bf16[1024,1024]{1,0:T(8,128)(2,1)S(1)} %get-tuple-element.14.wout_ref, f32[1,1024]{1,0:T(1,128)S(1)} %bitcast.15, f32[1,1024]{1,0:T(1,128)S(1)} %bitcast.16, ...), custom_call_target="tpu_custom_call" | custom-call | flops 1000000000 | bytes 1000000 | tf_op jit(solution)/shard_map/back/pallas_call | solution.py:238
  (5 shorter events, 0.0 us)
Async XLA Ops:
  0.0 0.9 copy-start.3
  0.9 18.6 %copy-start = (bf16[1024,3072]{1,0:T(8,128)(2,1)S(1)}, bf16[1024,3072]{1,0:T(8,128)(2,1)}, u32[]{:S(2)}) copy-start(bf16[1024,3072]{1,0:T(8,128)(2,1)} %wqkv_ref.1) | copy-start | bytes 18874372
  0.9 18.6 %copy-start.1 = (bf16[256,1024]{1,0:T(8,128)(2,1)S(1)}, bf16[256,1024]{1,0:T(8,128)(2,1)}, u32[]{:S(2)}) copy-start(bf16[256,1024]{1,0:T(8,128)(2,1)} %pos_ref.1) | copy-start | bytes 1572868
  0.9 18.6 %copy-start.2 = (bf16[216,1024]{1,0:T(8,128)(2,1)S(1)}, bf16[216,1024]{1,0:T(8,128)(2,1)}, u32[]{:S(2)}) copy-start(bf16[216,1024]{1,0:T(8,128)(2,1)} %stem_ref.1) | copy-start | bytes 1327108
  0.9 18.6 %copy-start.4 = (f32[4,64,64]{2,1,0:T(8,128)S(1)}, f32[4,64,64]{2,1,0:T(8,128)}, u32[]{:S(2)}) copy-start(f32[4,64,64]{2,1,0:T(8,128)} %mid_ref.1) | copy-start | bytes 196612
  0.9 18.6 %copy-start.6 = (f32[3072]{0:T(1024)S(1)}, f32[3072]{0:T(1024)}, u32[]{:S(2)}) copy-start(f32[3072]{0:T(1024)} %param.23) | copy-start | bytes 36868
  0.9 18.6 %copy-start.7 = (f32[1024]{0:T(1024)S(1)}, f32[1024]{0:T(1024)}, u32[]{:S(2)}) copy-start(f32[1024]{0:T(1024)} %param.18) | copy-start | bytes 12292
  0.9 18.6 %copy-start.8 = (f32[1024]{0:T(1024)S(1)}, f32[1024]{0:T(1024)}, u32[]{:S(2)}) copy-start(f32[1024]{0:T(1024)} %param.20) | copy-start | bytes 12292
  0.9 18.6 %copy-start.9 = (f32[1024]{0:T(1024)S(1)}, f32[1024]{0:T(1024)}, u32[]{:S(2)}) copy-start(f32[1024]{0:T(1024)} %param.21) | copy-start | bytes 12292
  19.6 40.1 %copy-start.14 = (bf16[1024,1024]{1,0:T(8,128)(2,1)S(1)}, bf16[1024,1024]{1,0:T(8,128)(2,1)}, u32[]{:S(2)}) copy-start(bf16[1024,1024]{1,0:T(8,128)(2,1)} %wout_hbm.1) | copy-start | bytes 6291460
  59.7 131.1 %copy-start.5 = (f32[4096]{0:T(1024)S(1)}, f32[4096]{0:T(1024)}, u32[]{:S(2)}) copy-start(f32[4096]{0:T(1024)} %param.29) | copy-start | bytes 49156
  59.7 131.1 %copy-start.10 = (f32[1024]{0:T(1024)S(1)}, f32[1024]{0:T(1024)}, u32[]{:S(2)}) copy-start(f32[1024]{0:T(1024)} %param.25) | copy-start | bytes 12292
  59.7 131.1 %copy-start.11 = (f32[1024]{0:T(1024)S(1)}, f32[1024]{0:T(1024)}, u32[]{:S(2)}) copy-start(f32[1024]{0:T(1024)} %param.26) | copy-start | bytes 12292
  59.7 131.1 %copy-start.12 = (f32[1024]{0:T(1024)S(1)}, f32[1024]{0:T(1024)}, u32[]{:S(2)}) copy-start(f32[1024]{0:T(1024)} %param.27) | copy-start | bytes 12292
  59.7 131.0 %copy-start.13 = (f32[1024]{0:T(1024)S(1)}, f32[1024]{0:T(1024)}, u32[]{:S(2)}) copy-start(f32[1024]{0:T(1024)} %param.31) | copy-start | bytes 12292
